TPU v7x, 32 devices: a whole 2x2x4 slice. The times are simulated.
32 devices in a mesh: mb: 4 (over z), tp: 2 (over y), dp: 4 (over x, core).
Axes of the slice: x: 2, y: 2, z: 4, core: 2. Of those that a mesh axis runs over, the one named last changes fastest.
Arguments:
- hidden: bfloat16 [4, 8, 512, 7168], P('dp', 'mb', None, 'tp'), may hold values from -6 to 6
- latent: bfloat16 [4, 8, 512, 512], P('dp', 'mb', None, 'tp'), may hold values from -6 to 6
- out_grad: bfloat16 [4, 8, 512, 16384], P('dp', 'mb', None, 'tp'), may hold values from -0.059814453 to 0.059814453
- up_weight: bfloat16 [512, 16384], P(None, 'tp'), may hold values from -0.046875 to 0.046875
- mb_tokens: int32 [4, 8], P('dp'), may hold values from 128 to 512, as said below
- slot_mb: int32 [4, 8], P('dp', 'mb'), may hold values from 0 to 7, each once within a row
Outputs:
- up_grad: float32 [512, 16384], P(('mb', 'dp'), 'tp')
- running_down: float32 [4, 7168, 512], P('mb', 'tp', 'dp')
Inputs may be any that keep to these rules, and one draw needn't show every extreme that they name: `mb_tokens`: each count is a multiple of 128; in every group some microbatch has exactly 512 tokens. `slot_mb`: each row is a permutation of the microbatch numbers.
All inputs are finite; a program needn't handle non-finite values.
Results may differ from a plain program's by a relative error of at most 0.005.
Values may be sent and summed in bfloat16 or wider, within the bound.
A program may use at most 128 MiB of HBM per device.

v0:
```python
import jax
import jax.numpy as jnp
from jax import lax
from jax.sharding import PartitionSpec as P


def carried_in(part, axis, combine, identity):
    place = lax.axis_index(axis)
    gathered = lax.all_gather(part, axis)
    state = jnp.zeros_like(part) + jnp.asarray(identity, part.dtype)

    def one(lap, state):
        return combine(state, lax.dynamic_index_in_dim(gathered, lap, 0, False))

    return lax.fori_loop(0, place, one, state)


def add_terms(earlier, later):
    return earlier + later


def local(hidden, latent, out_grad, up_weight, mb_tokens, slot_mb):
    slot_count = hidden.shape[1]
    capacity = hidden.shape[2]
    micro_count = mb_tokens.shape[1]
    row_total = slot_count * capacity
    slot_ids = slot_mb[0]
    lookup = slot_ids[:, None] == jnp.arange(micro_count, dtype=jnp.int32)[None, :]
    counts = jnp.sum(jnp.where(lookup, mb_tokens[0][None, :], 0), axis=1)
    valid_rows = jnp.arange(capacity, dtype=jnp.int32)[None, :] < counts[:, None]
    masked_grads = jnp.where(valid_rows[:, :, None], out_grad[0], jnp.zeros((), out_grad.dtype))
    masked_grads = masked_grads.reshape(row_total, -1)
    factors = lax.all_gather(latent[0].reshape(row_total, -1), "tp", axis=1, tiled=True)
    partial_latent = lax.dot_general(
        masked_grads, up_weight, (((1,), (1,)), ((), ())), preferred_element_type=jnp.float32
    )
    latent_grad = lax.psum(partial_latent, "tp").astype(jnp.bfloat16)
    up_grad = lax.psum_scatter(
        lax.dot_general(
            factors, masked_grads, (((0,), (0,)), ((), ())), preferred_element_type=jnp.float32
        ),
        ("mb", "dp"),
        scatter_dimension=0,
        tiled=True,
    )
    hidden_rows = hidden[0].reshape(row_total, -1)
    down_term = lax.dot_general(
        hidden_rows, latent_grad, (((0,), (0,)), ((), ())), preferred_element_type=jnp.float32
    )
    down_share = lax.psum_scatter(down_term, "dp", scatter_dimension=1, tiled=True)
    earlier = carried_in(down_share, "mb", add_terms, jnp.zeros_like(down_share))
    running = earlier + down_share
    return (up_grad, running[None])


def solution(mesh):
    return jax.shard_map(
        local,
        mesh=mesh,
        in_specs=(
            P("dp", "mb", None, "tp"),
            P("dp", "mb", None, "tp"),
            P("dp", "mb", None, "tp"),
            P(None, "tp"),
            P("dp", None),
            P("dp", "mb"),
        ),
        out_specs=(P(("mb", "dp"), "tp"), P("mb", "tp", "dp")),
        check_vma=False,
    )
```

profile of v0, /device:TPU:26, one launch (start us, length us, event | category | flops | bytes accessed | tf_op | source)
XLA Modules:
  0.0 483.6 jit_solution(6459500900742012512)
XLA Ops:
  8.0 0.9 fusion.1
  8.9 0.1 iota_compare_fusion
  9.0 14.0 %bitcast_select_fusion = bf16[1024,8192]{1,0:T(8,128)(2,1)} fusion(bf16[1,2,512,8192]{3,2,1,0:T(8,128)(2,1)} %param.10, pred[1024]{0:T(1024)(128)(4,1)S(1)} %lt.30), kind=kLoop, calls=%fused_computation.1 | loop fusion | flops 8388608 | bytes 33555456 | tf_op jit(solution)/shard_map/jit(_where)/select_n | solution.py:31
  23.0 14.4 %fusion.2 = f32[1024,512]{1,0:T(8,128)S(1)} fusion(bf16[1024,8192]{1,0:T(8,128)(2,1)} %bitcast_select_fusion, bf16[512,8192]{1,0:T(8,128)(2,1)} %param.11), kind=kOutput, calls=%fused_computation.9 | convolution fusion | flops 8589934592 | bytes 27262976 | tf_op jit(solution)/shard_map/dot_general | solution.py:34
  37.4 52.7 %all-reduce.1 = bf16[1024,512]{1,0:T(8,128)(2,1)S(1)} all-reduce(f32[1024,512]{1,0:T(8,128)S(1)} %fusion.2), channel_id=1, replica_groups=mesh['mb'=4,'tp'=2,'dp'=4] {'tp'}, use_global_device_ids=true, to_apply=%region_2.3 | all-reduce | flops 524288 | bytes 3145728 | tf_op jit(solution)/shard_map/psum | solution.py:37
  90.2 9.2 %convolution_bitcast_fusion.1 = f32[3584,512]{0,1:T(8,128)} fusion(bf16[1024,3584]{1,0:T(8,128)(2,1)} %bitcast.25, bf16[1024,512]{1,0:T(8,128)(2,1)S(1)} %all-reduce.1), kind=kOutput, calls=%fused_computation.3 | convolution fusion | flops 3758096384 | bytes 15728640 | tf_op jit(solution)/shard_map/dot_general | solution.py:47
  99.4 0.0 all-gather.4.cloned.1.call-start
  99.4 0.5 all-gather.4.cloned.1.call-update
  99.9 0.0 all-gather.6.cloned.1.call-start
  100.0 64.5 %reduce-scatter.5.cloned.1.call-done = f32[3584,128]{0,1:T(8,128)} async-done(((f32[3584,512]{0,1:T(8,128)}), f32[3584,128]{0,1:T(8,128)}) %reduce-scatter.5.cloned.1.call-update) | async-done | bytes 1835024 | tf_op jit(solution)/shard_map/reduce_scatter | solution.py:50
  164.6 0.0 reduce-scatter.7.cloned.1.call-start
  164.6 16.0 %convolution_bitcast_fusion = f32[512,8192]{0,1:T(8,128)} fusion(bf16[1024,8192]{1,0:T(8,128)(2,1)} %bitcast_select_fusion, bf16[1024,512]{1,0:T(8,128)(2,1)} %all-gather.4.cloned.1.call-done), kind=kOutput, calls=%fused_computation.2 | convolution fusion | flops 8589934592 | bytes 34603008 | tf_op jit(solution)/shard_map/dot_general | solution.py:39
  180.6 17.5 %copy.21 = f32[512,8192]{1,0:T(8,128)} copy(f32[512,8192]{0,1:T(8,128)} %convolution_bitcast_fusion) | data formatting | bytes 33554432
  198.1 97.0 %all-gather.6.cloned.1.call-done = f32[14336,128]{0,1:T(8,128)} async-done(((f32[3584,128]{0,1:T(8,128)}), f32[14336,128]{0,1:T(8,128)}) %all-gather.6.cloned.1.call-update) | async-done | bytes 7340048 | tf_op jit(solution)/shard_map/all_gather | solution.py:9
  295.1 8.6 %copy.20 = f32[14336,128]{1,0:T(8,128)} copy(f32[14336,128]{0,1:T(8,128)} %all-gather.6.cloned.1.call-done) | data formatting | bytes 14680064 | tf_op jit(solution)/shard_map/while | solution.py:15
  303.7 0.1 broadcast_in_dim.41
  303.8 6.7 %while.10 = (s32[]{:T(128)}, f32[3584,128]{1,0:T(8,128)S(1)}, s32[]{:T(128)}, f32[4,3584,128]{2,1,0:T(8,128)}, s32[]{:T(128)}, /*index=5*/s32[]{:T(128)}, s32[]{:T(128)}) while((s32[]{:T(128)}, f32[3584,128]{1,0:T(8,128)S(1)}, s32[]{:T(128)}, f32[4,3584,128]{2,1,0:T(8,128)}, s32[]{:T(128)}, /*index=5*/s32[]{:T(128)}, s32[]{:T(128)}) %tuple.39), condition=%wide.region_5.6_spmd, body=%wide.region_4.5_spmd.sunk | while | flops 458757 | bytes 5505139 | solution.py:15
  303.9 1.9 bitcast_add_fusion.2
  305.8 2.4 bitcast_add_fusion.2
  308.2 2.3 bitcast_add_fusion.2
  310.5 1.7 copy.17
  312.2 2.9 add_bitcast_fusion
  315.1 1.7 copy.19
  316.8 159.2 %reduce-scatter.7.cloned.1.call-done = f32[32,8192]{1,0:T(8,128)} async-done(((f32[512,8192]{1,0:T(8,128)}), f32[32,8192]{1,0:T(8,128)}) %reduce-scatter.7.cloned.1.call-update) | async-done | bytes 1048592
  (6 shorter events, 0.1 us)
Async XLA Ops:
  8.0 156.5 %reduce-scatter.5.cloned.1.call-start = ((), (), s32[]{:S(2)}) async-start(), calls=%async_computation.3 | async-start | bytes 9175040 | tf_op jit(solution)/shard_map/reduce_scatter | solution.py:50
  99.4 65.3 %all-gather.4.cloned.1.call-start = ((), (), s32[]{:S(2)}) async-start(), calls=%async_computation.2 | async-start | bytes 1572864 | tf_op jit(solution)/shard_map/all_gather | solution.py:33
  99.9 195.1 %all-gather.6.cloned.1.call-start = ((), (), s32[]{:S(2)}) async-start(), calls=%async_computation.4 | async-start | bytes 9175040 | tf_op jit(solution)/shard_map/all_gather | solution.py:9
  164.6 311.4 %reduce-scatter.7.cloned.1.call-start = ((), (), s32[]{:S(2)}) async-start(), calls=%async_computation.5 | async-start | bytes 17825792
Sparse Core Ops, SparseCore 0:
  99.5 64.9 reduce-scatter.4
Sparse Core Ops, SparseCore 1:
  101.4 21.1 all-gather.3
  164.6 130.4 all-gather.5
  299.6 176.3 reduce-scatter.6
where the time goes:
time: 488 us; the launch traced here: 484 us
  waiting for transfers between devices  321 us (66%)
  blocking collectives  52.7 us (11%)
  matrix products  39.6 us (8%)
  local copies, waits for them, and re-layouts  29.6 us (6%)
  other arithmetic  24.4 us (5%)
  between operations  15.7 us (3%)
    unnamed x5, waiting for transfers between devices  160 us
    all_gather x1, waiting for transfers between devices, carried_in(): gathered = lax.all_gather(part, axis)  97 us
    reduce_scatter x1, waiting for transfers between devices, local(): lax.psum_scatter(down_term, 'dp', scatter_dimension=1, tiled=True)  64.5 us
    psum x1, blocking collectives, local(): latent_grad = lax.psum(partial_latent, 'tp').astype(jnp.bfloat16)  52.7 us
    unnamed x2, local copies, waits for them, and re-layouts  19.2 us
    dot_general x1, matrix products, local(): lax.dot_general(factors, masked_grads, (((0,), (0,)), ((), ())), preferre...  16 us
    dot_general x1, matrix products, local(): lax.dot_general(masked_grads, up_weight, (((1,), (1,)), ((), ())), prefer...  14.4 us
    select_n x1, other arithmetic, local(): jnp.where(valid_rows[:, :, None], out_grad[0], jnp.zeros((), out_grad.dty...  14 us
  transfers between devices with their start and end apart: 4, of which 3 were waited for; matrix products, arithmetic and copies ran while one was open for 11% of the time, Pallas kernels for 0%

commit v1 on v0

v1 whole, which is shorter than its diff:
```python
import functools

import jax
import jax.numpy as jnp
from jax import lax
from jax.experimental import pallas as pl
from jax.experimental.pallas import tpu as pltpu
from jax.sharding import PartitionSpec as P

F32 = jnp.float32
BF16 = jnp.bfloat16
UP_CHUNKS = 8
DOWN_CHUNKS = 7


def bits_of(size):
    count = size.bit_length() - 1
    assert size == 1 << count, "axis size"
    return count


def kernel(sizes, hidden, latent, grad, weight, tokens, slots, up_out, run_out,
           grad_v, weight_v, hidden_v, lat_v, lat_t, lg_acc, lg_send, lg_recv, lg_t,
           up, up_r, dn, dn_r, pre_r, pre_s,
           grad_sem, weight_sem, hidden_sem, lat_sem, lat_ss, lat_rs, lg_ss, lg_rs,
           up_ss, up_rs, dn_ss, dn_rs, pre_ss, pre_rs):
    n_mb, n_tp, n_dp = sizes
    mb, tp, dp = (lax.axis_index(a) for a in ("mb", "tp", "dp"))
    up_chunks, slot_count, cap, width = grad_v.shape
    rows = slot_count * cap
    rank_part = lat_v.shape[-1]
    down_chunks, down_width = dn.shape[0], dn.shape[-1]

    steps = []
    for axis, index, size in (("dp", dp, n_dp), ("mb", mb, n_mb)):
        for k in range(bits_of(size)):
            bit = (index // (1 << k)) % 2
            steps.append((bit, {axis: index + (1 - 2 * bit) * (1 << k)}))
    n_dp_steps = bits_of(n_dp)
    tp_peers = [{"tp": (tp + s) % n_tp} for s in range(1, n_tp)]
    following, preceding = {"mb": (mb + 1) % n_mb}, {"mb": (mb + n_mb - 1) % n_mb}

    def grad_copy(c):
        return pltpu.make_async_copy(
            grad.at[0, :, :, pl.ds(pl.multiple_of(c * width, width), width)], grad_v.at[c], grad_sem.at[c])

    def weight_copy(c):
        return pltpu.make_async_copy(
            weight.at[:, pl.ds(pl.multiple_of(c * width, width), width)], weight_v.at[c % 2], weight_sem.at[c % 2])

    def hidden_copy(c):
        return pltpu.make_async_copy(
            hidden.at[0, :, :, pl.ds(pl.multiple_of(c * down_width, down_width), down_width)],
            hidden_v.at[c % 2], hidden_sem.at[c % 2])

    def remote(src, dst, ss, rs, to):
        return pltpu.make_async_remote_copy(
            src_ref=src, dst_ref=dst, send_sem=ss, recv_sem=rs,
            device_id=to, device_id_type=pl.DeviceIdType.MESH)

    own_latent = pltpu.make_async_copy(latent.at[0], lat_v.at[0], lat_sem)
    own_latent.start()
    for c in range(2):
        weight_copy(c).start()
        hidden_copy(c).start()

    @pl.loop(0, up_chunks)
    def _(c):
        grad_copy(c).start()

    barrier = pltpu.get_barrier_semaphore()
    greeted = [to for _, to in steps] + tp_peers + [following, preceding]
    for to in greeted:
        pl.semaphore_signal(barrier, inc=1, device_id=to, device_id_type=pl.DeviceIdType.MESH)
    pl.semaphore_wait(barrier, len(greeted))

    def lat_copy(s):
        return remote(latent.at[0], lat_v.at[s], lat_ss.at[s - 1], lat_rs.at[s - 1], tp_peers[s - 1])

    def lg_copy(s):
        return remote(lg_send, lg_recv.at[s - 1], lg_ss.at[s - 1], lg_rs.at[s - 1], tp_peers[s - 1])

    for s in range(1, n_tp):
        lat_copy(s).start()

    def up_copy(k, c):
        bit, to = steps[k]
        src = (up if k == 0 else up_r[k - 1]).at[c]
        index = (slice(None),) * (len(steps) - 1 - k) + (1 - bit,)
        return remote(src.at[index], up_r[k].at[c], up_ss.at[k, c], up_rs.at[k, c], to)

    def up_kept(k, c):
        bit, _ = steps[k]
        src = up if k == 0 else up_r[k - 1]
        return src[(c,) + (slice(None),) * (len(steps) - 1 - k) + (bit,)].astype(F32)

    def up_add(k, c):
        up_copy(k, c).wait_recv()
        return up_kept(k, c) + up_r[k][c].astype(F32)

    def up_pass(k, c):
        up_r[k][c] = up_add(k, c).astype(BF16)
        up_copy(k + 1, c).start()

    def dn_copy(k, c):
        bit, to = steps[k]
        src = (dn if k == 0 else dn_r[k - 1]).at[c]
        index = (slice(None),) * (n_dp_steps - 1 - k) + (1 - bit,)
        return remote(src.at[index], dn_r[k].at[c], dn_ss.at[k, c], dn_rs.at[k, c], to)

    def dn_add(k, c):
        bit, _ = steps[k]
        dn_copy(k, c).wait_recv()
        src = dn if k == 0 else dn_r[k - 1]
        kept = src[(c,) + (slice(None),) * (n_dp_steps - 1 - k) + (bit,)]
        return kept.astype(F32) + dn_r[k][c].astype(F32)

    def dn_pass(k, c):
        dn_r[k][c] = dn_add(k, c).astype(BF16)
        dn_copy(k + 1, c).start()

    def pre_copy(c):
        return remote(pre_s.at[c], pre_r.at[c], pre_ss.at[c], pre_rs.at[c], following)

    counts = [tokens[0, slots[0, s]] for s in range(slot_count)]

    def live(shape):
        row = lax.broadcasted_iota(jnp.int32, shape, 0)
        valid = row < counts[0]
        for s in range(1, slot_count):
            valid = valid | ((row >= s * cap) & (row < s * cap + counts[s]))
        return valid

    lg_acc[...] = jnp.zeros_like(lg_acc)

    @pl.loop(0, up_chunks)
    def _(c):
        grad_copy(c).wait()
        weight_copy(c).wait()
        lg_acc[...] += lax.dot_general(
            grad_v[c].reshape(rows, width), weight_v[c % 2], (((1,), (1,)), ((), ())),
            preferred_element_type=F32)

        @pl.when(c + 2 < up_chunks)
        def _():
            weight_copy(c + 2).start()

    lg_send[...] = lg_acc[...].astype(BF16)
    for s in range(1, n_tp):
        lg_copy(s).start()

    own_latent.wait()
    for s in range(1, n_tp):
        lat_copy(s).wait_recv()
    for s in range(n_tp):
        part = lat_v[s].reshape(rows, rank_part).astype(F32)
        part = jnp.where(live(part.shape), part, 0.0)
        home = (tp + n_tp - s) % n_tp
        lat_t[home] = part.T.astype(BF16)

    def up_first(c):
        up_pass(0, c)

    @pl.loop(0, up_chunks)
    def _(c):
        block = lax.dot_general(
            lat_t[...].reshape(n_tp * rank_part, rows), grad_v[c].reshape(rows, width),
            (((1,), (0,)), ((), ())), preferred_element_type=F32)
        up[c] = block.astype(BF16).reshape(up.shape[1:])
        up_copy(0, c).start()

        @pl.when(c > 0)
        def _():
            up_first(c - 1)

    up_first(up_chunks - 1)

    total = lg_acc[...]
    for s in range(1, n_tp):
        lg_copy(s).wait_recv()
        total = total + lg_recv[s - 1].astype(F32)
    total = jnp.where(live(total.shape), total, 0.0)
    lg_t[...] = total.T.astype(BF16)

    @pl.loop(0, down_chunks)
    def _(c):
        hidden_copy(c).wait()
        block = lax.dot_general(
            lg_t[...], hidden_v[c % 2].reshape(rows, down_width),
            (((1,), (0,)), ((), ())), preferred_element_type=F32)
        dn[c] = block.astype(BF16).reshape(dn.shape[1:])
        dn_copy(0, c).start()

        @pl.when(c + 2 < down_chunks)
        def _():
            hidden_copy(c + 2).start()

        @pl.when(c > 0)
        def _():
            dn_pass(0, c - 1)

    dn_pass(0, down_chunks - 1)

    last = len(steps) - 1

    @pl.loop(0, up_chunks + last - 1)
    def _(t):
        for k in range(1, last + 1):
            c = t - (k - 1)

            @pl.when((c >= 0) & (c < up_chunks))
            def _():
                if k < last:
                    up_pass(k, c)
                else:
                    at = pl.ds(pl.multiple_of(c * width, width), width)
                    up_out[:, at] = up_add(k, c)

    for k in range(1, n_dp_steps - 1):
        @pl.loop(0, down_chunks)
        def _(c):
            dn_pass(k, c)

    @pl.loop(0, down_chunks)
    def _(c):
        share = dn_add(n_dp_steps - 1, c)
        at = pl.ds(pl.multiple_of(c * down_width, down_width), down_width)

        @pl.when(mb == 0)
        def _():
            pre_s[c] = share.astype(BF16)
            pre_copy(c).start()
            run_out[0, at, :] = share.T

        @pl.when(mb > 0)
        def _():
            pre_copy(c).wait_recv()
            running = share + pre_r[c].astype(F32)

            @pl.when(mb < n_mb - 1)
            def _():
                pre_s[c] = running.astype(BF16)
                pre_copy(c).start()

            run_out[0, at, :] = running.T

    for s in range(1, n_tp):
        lat_copy(s).wait_send()
        lg_copy(s).wait_send()

    @pl.loop(0, up_chunks)
    def _(c):
        for k in range(len(steps)):
            up_copy(k, c).wait_send()

    @pl.loop(0, down_chunks)
    def _(c):
        for k in range(n_dp_steps):
            dn_copy(k, c).wait_send()

        @pl.when(mb < n_mb - 1)
        def _():
            pre_copy(c).wait_send()


def local(sizes, hidden, latent, out_grad, up_weight, mb_tokens, slot_mb):
    n_mb, n_tp, n_dp = sizes
    _, slot_count, cap, feature_part = hidden.shape
    rank_part = latent.shape[3]
    rank, column_part = up_weight.shape
    rows = slot_count * cap
    width = column_part // UP_CHUNKS
    down_width = feature_part // DOWN_CHUNKS
    dp_bits, mb_bits = bits_of(n_dp), bits_of(n_mb)
    bits = dp_bits + mb_bits
    up_rows = rank >> bits
    share = rank >> dp_bits
    dma = pltpu.SemaphoreType.DMA
    scratch = [
        pltpu.VMEM((UP_CHUNKS, slot_count, cap, width), BF16),
        pltpu.VMEM((2, rank, width), BF16),
        pltpu.VMEM((2, slot_count, cap, down_width), BF16),
        pltpu.VMEM((n_tp, slot_count, cap, rank_part), BF16),
        pltpu.VMEM((n_tp, rank_part, rows), BF16),
        pltpu.VMEM((rows, rank), F32),
        pltpu.VMEM((rows, rank), BF16),
        pltpu.VMEM((n_tp - 1, rows, rank), BF16),
        pltpu.VMEM((rank, rows), BF16),
        pltpu.VMEM((UP_CHUNKS,) + (2,) * bits + (up_rows, width), BF16),
        [pltpu.VMEM((UP_CHUNKS,) + (2,) * (bits - 1 - k) + (up_rows, width), BF16) for k in range(bits)],
        pltpu.VMEM((DOWN_CHUNKS,) + (2,) * dp_bits + (share, down_width), BF16),
        [pltpu.VMEM((DOWN_CHUNKS,) + (2,) * (dp_bits - 1 - k) + (share, down_width), BF16) for k in range(dp_bits)],
        pltpu.VMEM((DOWN_CHUNKS, share, down_width), BF16),
        pltpu.VMEM((DOWN_CHUNKS, share, down_width), BF16),
        dma((UP_CHUNKS,)), dma((2,)), dma((2,)), dma,
        dma((n_tp - 1,)), dma((n_tp - 1,)), dma((n_tp - 1,)), dma((n_tp - 1,)),
        dma((bits, UP_CHUNKS)), dma((bits, UP_CHUNKS)),
        dma((dp_bits, DOWN_CHUNKS)), dma((dp_bits, DOWN_CHUNKS)),
        dma((DOWN_CHUNKS,)), dma((DOWN_CHUNKS,)),
    ]
    hbm = pl.BlockSpec(memory_space=pl.ANY)
    smem = pl.BlockSpec(memory_space=pltpu.SMEM)
    vmem = pl.BlockSpec(memory_space=pltpu.VMEM)
    return pl.pallas_call(
        functools.partial(kernel, sizes),
        out_shape=(
            jax.ShapeDtypeStruct((up_rows, column_part), F32),
            jax.ShapeDtypeStruct((1, feature_part, share), F32),
        ),
        in_specs=[hbm] * 4 + [smem] * 2,
        out_specs=(vmem, vmem),
        scratch_shapes=scratch,
        compiler_params=pltpu.CompilerParams(
            collective_id=0, has_side_effects=True, vmem_limit_bytes=67043328),
    )(hidden, latent, out_grad, up_weight, mb_tokens, slot_mb)


def solution(mesh):
    sizes = tuple(mesh.shape[axis] for axis in ("mb", "tp", "dp"))
    return jax.shard_map(
        functools.partial(local, sizes),
        mesh=mesh,
        in_specs=(
            P("dp", "mb", None, "tp"),
            P("dp", "mb", None, "tp"),
            P("dp", "mb", None, "tp"),
            P(None, "tp"),
            P("dp", None),
            P("dp", "mb"),
        ),
        out_specs=(P(("mb", "dp"), "tp"), P("mb", "tp", "dp")),
        check_vma=False,
    )
```

time: 488 us -> 125 us (0.26)
  waiting for transfers between devices: 321 us -> 0 us
  Pallas kernels: 0 us -> 119 us
  blocking collectives: 52.7 us -> 0 us
  matrix products: 39.6 us -> 0 us
  local copies, waits for them, and re-layouts: 29.6 us -> 5.11 us
  other arithmetic: 24.4 us -> 0 us
  between operations: 15.7 us -> 0.64 us
    unnamed x5 -> x0, waiting for transfers between devices: 160 us -> none
    pallas_call x0 -> x1, Pallas kernels: none -> 119 us  [local(): pl.pallas_call(functools.partial(kernel, sizes), out_shape=(jax.ShapeDtyp...]
    all_gather x2 -> x0, waiting for transfers between devices: 97 us -> none  [the longest x1 97 us: carried_in(): gathered = lax.all_gather(part, axis)]
    reduce_scatter x1 -> x0, waiting for transfers between devices: 64.5 us -> none  [local(): lax.psum_scatter(down_term, 'dp', scatter_dimension=1, tiled=True)]
    psum x1 -> x0, blocking collectives: 52.7 us -> none  [local(): latent_grad = lax.psum(partial_latent, 'tp').astype(jnp.bfloat16)]
    dot_general x3 -> x0, matrix products: 39.6 us -> none  [the longest x1 16 us: local(): lax.dot_general(factors, masked_grads, (((0,), (0,)), ((), ())), preferre...]
    unnamed x2, local copies, waits for them, and re-layouts: 19.2 us -> 5.11 us
    select_n x1 -> x0, other arithmetic: 14 us -> none  [local(): jnp.where(valid_rows[:, :, None], out_grad[0], jnp.zeros((), out_grad.dty...]
  transfers between devices with their start and end apart: 4 -> 0, of which waited for: 3 -> 0; matrix products, arithmetic and copies ran while one was open for 11% -> 0% of each run, Pallas kernels for 0% -> 0%
where the time goes in v1:
time: 125 us
  Pallas kernels  119 us (95%)
  local copies, waits for them, and re-layouts  5.11 us (4%)
    pallas_call x1, Pallas kernels, local(): pl.pallas_call(functools.partial(kernel, sizes), out_shape=(jax.ShapeDtyp...  119 us
    unnamed x2, local copies, waits for them, and re-layouts  5.11 us

profile of v1, /device:TPU:26, one launch (start us, length us, event | category | flops | bytes accessed | tf_op | source)
XLA Modules:
  0.0 125.0 jit_solution(7239867497434794284)
XLA Ops:
  0.6 119.2 %shard_map.77 = (f32[32,8192]{1,0:T(8,128)}, f32[1,3584,128]{2,1,0:T(8,128)}) custom-call(bf16[1,2,512,3584]{3,2,1,0:T(8,128)(2,1)} %hidden.1, bf16[1,2,512,256]{3,2,1,0:T(8,128)(2,1)} %latent.1, bf16[1,2,512,8192]{3,2,1,0:T(8,128)(2,1)} %grad.1, bf16[512,8192]{1,0:T(8,128)(2,1)} %weight.1, s32[1,8]{1,0:T(1,128)} %tokens.1, s32[1,2]{1,0:T(1,128)} %slots.1), custom_call_target="tpu_custom_call" | custom-call | tf_op jit(solution)/shard_map/pallas_call | solution.py:304
  119.9 2.3 %copy.10 = f32[32,8192]{1,0:T(8,128)} copy(f32[32,8192]{1,0:T(8,128)} %get-tuple-element.4) | data formatting | bytes 2097152
  122.1 2.8 %copy.11 = f32[1,3584,128]{2,1,0:T(8,128)} copy(f32[1,3584,128]{2,1,0:T(8,128)} %get-tuple-element.5) | data formatting | bytes 3670016

commit v2 on v1

--- a/solution.py
+++ b/solution.py
@@ -83,24 +83,64 @@
     for s in range(1, n_tp):
         lat_copy(s).start()
 
-    def up_copy(k, c):
+    tp_bits = bits_of(n_tp)
+    last = len(steps) - 1
+    part_steps = len(steps) - tp_bits
+
+    def part_at(s):
+        part = (tp + n_tp - s) % n_tp
+        return tuple((part // (1 << k)) % 2 for k in reversed(range(tp_bits)))
+
+    def up_copy(k, s, c):
         bit, to = steps[k]
-        src = (up if k == 0 else up_r[k - 1]).at[c]
-        index = (slice(None),) * (len(steps) - 1 - k) + (1 - bit,)
-        return remote(src.at[index], up_r[k].at[c], up_ss.at[k, c], up_rs.at[k, c], to)
-
-    def up_kept(k, c):
+        head = (c,) + (part_at(s) if k < part_steps else ())
+        free = len(steps) - 1 - k - (len(head) - 1)
+        src = (up if k == 0 else up_r[k - 1]).at[head + (slice(None),) * free + (1 - bit,)]
+        return remote(src, up_r[k].at[head], up_ss.at[k, s, c], up_rs.at[k, s, c], to)
+
+    def up_add(k, s, c):
         bit, _ = steps[k]
-        src = up if k == 0 else up_r[k - 1]
-        return src[(c,) + (slice(None),) * (len(steps) - 1 - k) + (bit,)].astype(F32)
-
-    def up_add(k, c):
-        up_copy(k, c).wait_recv()
-        return up_kept(k, c) + up_r[k][c].astype(F32)
-
-    def up_pass(k, c):
-        up_r[k][c] = up_add(k, c).astype(BF16)
-        up_copy(k + 1, c).start()
+        head = (c,) + (part_at(s) if k < part_steps else ())
+        free = len(steps) - 1 - k - (len(head) - 1)
+        up_copy(k, s, c).wait_recv()
+        kept = (up if k == 0 else up_r[k - 1])[head + (slice(None),) * free + (bit,)]
+        return kept.astype(F32) + up_r[k][head].astype(F32)
+
+    def up_pass(k, s, c):
+        head = (c,) + (part_at(s) if k < part_steps else ())
+        up_r[k][head] = up_add(k, s, c).astype(BF16)
+        if k + 1 != part_steps:
+            up_copy(k + 1, s, c).start()
+
+    def up_make(s, c):
+        block = lax.dot_general(
+            lat_t[s], grad_v[c].reshape(rows, width),
+            (((1,), (0,)), ((), ())), preferred_element_type=F32).astype(BF16)
+        head = (c,) + part_at(s)
+        up[head] = block.reshape(up.shape[1 + tp_bits:])
+        up_copy(0, s, c).start()
+
+    def up_tick(t):
+        for k in range(1, last + 1):
+            c = t - (k - 1)
+
+            @pl.when((c >= 0) & (c < up_chunks))
+            def _():
+                if k < part_steps:
+                    for s in range(1 if k == 1 else 0, n_tp):
+                        up_pass(k, s, c)
+                    if k + 1 == part_steps:
+                        up_copy(part_steps, 0, c).start()
+                elif k < last:
+                    up_pass(k, 0, c)
+                else:
+                    at = pl.ds(pl.multiple_of(c * width, width), width)
+                    up_out[:, at] = up_add(k, 0, c)
+
+    def latent_part(s):
+        part = lat_v[s].reshape(rows, rank_part).astype(F32)
+        part = jnp.where(live(part.shape), part, 0.0)
+        lat_t[s] = part.T.astype(BF16)
 
     def dn_copy(k, c):
         bit, to = steps[k]
@@ -131,11 +171,24 @@
             valid = valid | ((row >= s * cap) & (row < s * cap + counts[s]))
         return valid
 
+    own_latent.wait()
+    latent_part(0)
+
+    @pl.loop(0, up_chunks)
+    def _(c):
+        grad_copy(c).wait()
+        up_make(0, c)
+
+        @pl.when(c > 0)
+        def _():
+            up_pass(0, 0, c - 1)
+
+    up_pass(0, 0, up_chunks - 1)
+
     lg_acc[...] = jnp.zeros_like(lg_acc)
 
     @pl.loop(0, up_chunks)
     def _(c):
-        grad_copy(c).wait()
         weight_copy(c).wait()
         lg_acc[...] += lax.dot_general(
             grad_v[c].reshape(rows, width), weight_v[c % 2], (((1,), (1,)), ((), ())),
@@ -145,35 +198,34 @@
         def _():
             weight_copy(c + 2).start()
 
+        @pl.when(c > 0)
+        def _():
+            up_pass(1, 0, c - 1)
+
     lg_send[...] = lg_acc[...].astype(BF16)
     for s in range(1, n_tp):
         lg_copy(s).start()
 
-    own_latent.wait()
     for s in range(1, n_tp):
         lat_copy(s).wait_recv()
-    for s in range(n_tp):
-        part = lat_v[s].reshape(rows, rank_part).astype(F32)
-        part = jnp.where(live(part.shape), part, 0.0)
-        home = (tp + n_tp - s) % n_tp
-        lat_t[home] = part.T.astype(BF16)
-
-    def up_first(c):
-        up_pass(0, c)
-
-    @pl.loop(0, up_chunks)
-    def _(c):
-        block = lax.dot_general(
-            lat_t[...].reshape(n_tp * rank_part, rows), grad_v[c].reshape(rows, width),
-            (((1,), (0,)), ((), ())), preferred_element_type=F32)
-        up[c] = block.astype(BF16).reshape(up.shape[1:])
-        up_copy(0, c).start()
-
-        @pl.when(c > 0)
-        def _():
-            up_first(c - 1)
-
-    up_first(up_chunks - 1)
+        latent_part(s)
+
+        @pl.loop(0, up_chunks)
+        def _(c):
+            up_make(s, c)
+
+            @pl.when(c > 0)
+            def _():
+                up_pass(0, s, c - 1)
+
+        up_pass(0, s, up_chunks - 1)
+
+    up_pass(1, 0, up_chunks - 1)
+    early = up_chunks - 2
+
+    @pl.loop(0, early)
+    def _(t):
+        up_tick(t)
 
     total = lg_acc[...]
     for s in range(1, n_tp):
@@ -201,20 +253,9 @@
 
     dn_pass(0, down_chunks - 1)
 
-    last = len(steps) - 1
-
-    @pl.loop(0, up_chunks + last - 1)
+    @pl.loop(early, up_chunks + last - 1)
     def _(t):
-        for k in range(1, last + 1):
-            c = t - (k - 1)
-
-            @pl.when((c >= 0) & (c < up_chunks))
-            def _():
-                if k < last:
-                    up_pass(k, c)
-                else:
-                    at = pl.ds(pl.multiple_of(c * width, width), width)
-                    up_out[:, at] = up_add(k, c)
+        up_tick(t)
 
     for k in range(1, n_dp_steps - 1):
         @pl.loop(0, down_chunks)
@@ -251,7 +292,8 @@
     @pl.loop(0, up_chunks)
     def _(c):
         for k in range(len(steps)):
-            up_copy(k, c).wait_send()
+            for s in range(n_tp if k < part_steps else 1):
+                up_copy(k, s, c).wait_send()
 
     @pl.loop(0, down_chunks)
     def _(c):
@@ -294,7 +336,7 @@
         pltpu.VMEM((DOWN_CHUNKS, share, down_width), BF16),
         dma((UP_CHUNKS,)), dma((2,)), dma((2,)), dma,
         dma((n_tp - 1,)), dma((n_tp - 1,)), dma((n_tp - 1,)), dma((n_tp - 1,)),
-        dma((bits, UP_CHUNKS)), dma((bits, UP_CHUNKS)),
+        dma((bits, n_tp, UP_CHUNKS)), dma((bits, n_tp, UP_CHUNKS)),
         dma((dp_bits, DOWN_CHUNKS)), dma((dp_bits, DOWN_CHUNKS)),
         dma((DOWN_CHUNKS,)), dma((DOWN_CHUNKS,)),
     ]

time: 125 us -> 119 us (0.952); the launches traced: 125 us -> 118 us
  Pallas kernels: 119 us -> 112 us
    pallas_call x1, Pallas kernels: 119 us -> 112 us  [local(): pl.pallas_call(functools.partial(kernel, sizes), out_shape=(jax.ShapeDtyp...]
where the time goes in v2:
time: 119 us; the launch traced here: 118 us
  Pallas kernels  112 us (94%)
  local copies, waits for them, and re-layouts  5.11 us (4%)
    pallas_call x1, Pallas kernels, local(): pl.pallas_call(functools.partial(kernel, sizes), out_shape=(jax.ShapeDtyp...  112 us
    unnamed x2, local copies, waits for them, and re-layouts  5.11 us

profile of v2, /device:TPU:26, one launch (start us, length us, event | category | flops | bytes accessed | tf_op | source)
XLA Modules:
  0.0 117.5 jit_solution(4091809537540323220)
XLA Ops:
  0.6 111.8 %shard_map.77 = (f32[32,8192]{1,0:T(8,128)}, f32[1,3584,128]{2,1,0:T(8,128)}) custom-call(bf16[1,2,512,3584]{3,2,1,0:T(8,128)(2,1)} %hidden.1, bf16[1,2,512,256]{3,2,1,0:T(8,128)(2,1)} %latent.1, bf16[1,2,512,8192]{3,2,1,0:T(8,128)(2,1)} %grad.1, bf16[512,8192]{1,0:T(8,128)(2,1)} %weight.1, s32[1,8]{1,0:T(1,128)} %tokens.1, s32[1,2]{1,0:T(1,128)} %slots.1), custom_call_target="tpu_custom_call" | custom-call | tf_op jit(solution)/shard_map/pallas_call | solution.py:346
  112.4 2.3 %copy.10 = f32[32,8192]{1,0:T(8,128)} copy(f32[32,8192]{1,0:T(8,128)} %get-tuple-element.4) | data formatting | bytes 2097152
  114.7 2.8 %copy.11 = f32[1,3584,128]{2,1,0:T(8,128)} copy(f32[1,3584,128]{2,1,0:T(8,128)} %get-tuple-element.5) | data formatting | bytes 3670016
